TPU v7x, 128 devices: a whole 4x4x4 slice. The times are simulated.
128 devices in a mesh: row: 8 (over z, y_hi), col: 16 (over x, y_lo, core).
Axes of the slice: x: 4, y: 4 (y_hi: 2, y_lo: 2; y = y_hi * 2 + y_lo), z: 4, core: 2. Of those that a mesh axis runs over, the one named last changes fastest.
Arguments:
- tri_panels: float32 [8192, 8192], P('row', 'col'), may hold values from -1 to 2, as said below
- rhs_rows: float32 [8192, 2048], P(('row', 'col')), may hold values from -6 to 6
Outputs:
- rhs_grid: float32 [8192, 2048], P('row', 'col')
Inputs may be any that keep to these rules, and one draw needn't show every extreme that they name: `tri_panels`: in L's row order the entries above the diagonal are zero and the diagonal entries are positive.
All inputs are finite; a program needn't handle non-finite values.
Results may differ from a plain program's by a relative error of at most 0.00011.
Values sent between devices are 32-bit elements; how exact they have to be, the bound alone decides.
A program may use at most 256 MiB of HBM per device.

v0:
```python
import jax
import jax.numpy as jnp
from jax import lax
from jax.sharding import PartitionSpec as P


def picked(array, axis, root):
    return lax.dynamic_index_in_dim(lax.all_gather(array, axis), root, 0, keepdims=False)


def on_device(tri_panels, rhs_rows):
    row_count = lax.axis_size("row")
    col_count = lax.axis_size("col")
    row_position = lax.axis_index("row")
    col_position = lax.axis_index("col")
    local_rows, block_size = tri_panels.shape
    blocks = local_rows // block_size
    sub_rows = block_size // col_count
    parted = rhs_rows.reshape(blocks, sub_rows, rhs_rows.shape[1])
    state_rhs = lax.all_to_all(parted, "col", split_axis=2, concat_axis=1, tiled=True)
    identity_block = jnp.eye(block_size, dtype=jnp.float32)
    own_pieces = tri_panels.reshape(blocks, block_size, block_size)
    own_diag = lax.dynamic_index_in_dim(own_pieces, col_position // row_count, 0, keepdims=False)
    own_diag = jnp.where(col_position % row_count == row_position, own_diag, identity_block)
    own_inverse = jax.scipy.linalg.solve_triangular(own_diag, identity_block, lower=True)

    def advance(state_rhs, panel_cols, inverse_block, step_index, first_slot):
        count = blocks - first_slot
        owner_row = step_index % row_count
        slot_index = step_index // row_count
        pieces = panel_cols.reshape(count, block_size, block_size)
        current = lax.dynamic_index_in_dim(state_rhs, slot_index, 0, keepdims=False)
        local_solution = jnp.dot(
            inverse_block,
            current,
            precision=lax.Precision.HIGHEST,
            preferred_element_type=jnp.float32,
        )
        solution = picked(local_solution, "row", owner_row)
        stored = jnp.where(row_position == owner_row, solution, current)
        state_rhs = lax.dynamic_update_index_in_dim(state_rhs, stored, slot_index, 0)
        global_block = (first_slot + jnp.arange(count, dtype=jnp.int32)) * row_count + row_position
        product = jnp.einsum("sij,jc->sic", pieces, solution, precision=lax.Precision.HIGHEST)
        trailing = state_rhs[first_slot:]
        trailing = jnp.where(
            (global_block > step_index)[:, None, None], trailing - product, trailing
        )
        if first_slot > 0:
            return jnp.concatenate([state_rhs[:first_slot], trailing], 0)
        return trailing

    group_count = (col_count + row_count - 1) // row_count
    everything, inverses = (
        lax.all_gather(tri_panels, "col", axis=1, tiled=True),
        lax.all_gather(own_inverse, "col", axis=1, tiled=True),
    )
    for first_slot in range(group_count):
        begin_step = first_slot * row_count
        end_step = min(begin_step + row_count, col_count)
        own_rows = everything[first_slot * block_size :]

        def upfront_step(step_index, state_rhs, own_rows=own_rows, first_slot=first_slot):
            panel_cols = lax.dynamic_slice_in_dim(own_rows, step_index * block_size, block_size, 1)
            inverse_block = lax.dynamic_slice_in_dim(
                inverses, step_index * block_size, block_size, 1
            )
            return advance(state_rhs, panel_cols, inverse_block, step_index, first_slot)

        state_rhs = lax.fori_loop(begin_step, end_step, upfront_step, state_rhs)
    return state_rhs.reshape(local_rows, state_rhs.shape[2])


def solution(mesh):
    return jax.shard_map(
        on_device,
        mesh=mesh,
        in_specs=(P("row", "col"), P(("row", "col"), None)),
        out_specs=P("row", "col"),
        check_vma=False,
    )
```

profile of v0, /device:TPU:0, one launch (start us, length us, event | category | flops | bytes accessed | tf_op | source)
XLA Modules:
  0.0 1225.2 jit_solution(3915089604845928567)
XLA Ops:
  9.3 11.6 while.33
  20.9 39.3 %custom-call.4 = f32[4,128,128]{1,2,0:T(8,128)S(1)} custom-call(f32[4,128,128]{2,1,0:T(8,128)S(1)} %get-tuple-element.290), custom_call_target="InvertDiagBlocksLowerTriangular" | custom-call | tf_op jit(solution)/shard_map/jit(_solve_triangular)/triangular_solve | solution.py:25
  76.7 14.4 %all-to-all-done = f32[16,1,8192]{2,1,0:T(1,128)S(1)} async-done(((f32[16,1,8192]{2,1,0:T(1,128)}), f32[16,1,8192]{2,1,0:T(1,128)S(1)}, u32[]{:S(2)}, u32[]{:S(2)}) %all-to-all-start) | async-done | bytes 524320 | tf_op jit(solution)/shard_map/all_to_all | solution.py:20
  96.2 91.5 %all-gather.13.cloned.1.call-done = f32[1024,8192]{1,0:T(8,128)} async-done(((f32[1024,512]{1,0:T(8,128)}), f32[1024,8192]{1,0:T(8,128)}) %all-gather.13.cloned.1.call-update) | async-done | bytes 33554448 | tf_op jit(solution)/shard_map/all_gather | solution.py:54
  187.7 11.5 slice.70
  199.2 82.4 %all-gather.11.cloned.1.call-done = f32[512,8192]{1,0:T(8,128)} async-done(((f32[512,512]{1,0:T(8,128)}), f32[512,8192]{1,0:T(8,128)}) %all-gather.11.cloned.1.call-update) | async-done | bytes 16777232 | tf_op jit(solution)/shard_map/all_gather | solution.py:55
  281.6 471.9 %while.31 = (s32[]{:T(128)}, f32[2,512,128]{2,1,0:T(8,128)S(1)}, s32[]{:T(128)}, f32[512,8192]{1,0:T(8,128)}, f32[1024,8192]{1,0:T(8,128)}, /*index=5*/s32[]{:T(...) while((s32[]{:T(128)}, f32[2,512,128]{2,1,0:T(8,128)S(1)}, ...), condition=%wide.region_1.2_spmd, body=%wide.region_0.1_spmd.sunk | while | flops 1208287232 | bytes 17039816 | solution.py:69
  286.3 53.0 %all-gather.15.cloned.1.call-done = f32[4096,128]{1,0:T(8,128)} async-done(((f32[512,128]{1,0:T(8,128)}), f32[4096,128]{1,0:T(8,128)}) %all-gather.15.cloned.1.call-update) | async-done | bytes 2097168 | tf_op jit(solution)/shard_map/while/body/eval_jaxpr/all_gather | solution.py:8
  348.1 49.8 %all-gather.15.cloned.1.call-done = f32[4096,128]{1,0:T(8,128)} async-done(((f32[512,128]{1,0:T(8,128)}), f32[4096,128]{1,0:T(8,128)}) %all-gather.15.cloned.1.call-update) | async-done | bytes 2097168 | tf_op jit(solution)/shard_map/while/body/eval_jaxpr/all_gather | solution.py:8
  406.7 49.8 %all-gather.15.cloned.1.call-done = f32[4096,128]{1,0:T(8,128)} async-done(((f32[512,128]{1,0:T(8,128)}), f32[4096,128]{1,0:T(8,128)}) %all-gather.15.cloned.1.call-update) | async-done | bytes 2097168 | tf_op jit(solution)/shard_map/while/body/eval_jaxpr/all_gather | solution.py:8
  465.3 49.8 %all-gather.15.cloned.1.call-done = f32[4096,128]{1,0:T(8,128)} async-done(((f32[512,128]{1,0:T(8,128)}), f32[4096,128]{1,0:T(8,128)}) %all-gather.15.cloned.1.call-update) | async-done | bytes 2097168 | tf_op jit(solution)/shard_map/while/body/eval_jaxpr/all_gather | solution.py:8
  523.9 49.8 %all-gather.15.cloned.1.call-done = f32[4096,128]{1,0:T(8,128)} async-done(((f32[512,128]{1,0:T(8,128)}), f32[4096,128]{1,0:T(8,128)}) %all-gather.15.cloned.1.call-update) | async-done | bytes 2097168 | tf_op jit(solution)/shard_map/while/body/eval_jaxpr/all_gather | solution.py:8
  582.5 49.8 %all-gather.15.cloned.1.call-done = f32[4096,128]{1,0:T(8,128)} async-done(((f32[512,128]{1,0:T(8,128)}), f32[4096,128]{1,0:T(8,128)}) %all-gather.15.cloned.1.call-update) | async-done | bytes 2097168 | tf_op jit(solution)/shard_map/while/body/eval_jaxpr/all_gather | solution.py:8
  641.1 49.8 %all-gather.15.cloned.1.call-done = f32[4096,128]{1,0:T(8,128)} async-done(((f32[512,128]{1,0:T(8,128)}), f32[4096,128]{1,0:T(8,128)}) %all-gather.15.cloned.1.call-update) | async-done | bytes 2097168 | tf_op jit(solution)/shard_map/while/body/eval_jaxpr/all_gather | solution.py:8
  699.8 49.8 %all-gather.15.cloned.1.call-done = f32[4096,128]{1,0:T(8,128)} async-done(((f32[512,128]{1,0:T(8,128)}), f32[4096,128]{1,0:T(8,128)}) %all-gather.15.cloned.1.call-update) | async-done | bytes 2097168 | tf_op jit(solution)/shard_map/while/body/eval_jaxpr/all_gather | solution.py:8
  753.5 464.0 %while.32 = (s32[]{:T(128)}, f32[2,512,128]{2,1,0:T(8,128)S(1)}, s32[]{:T(128)}, f32[512,8192]{1,0:T(8,128)}, s32[1]{0:T(128)}, /*index=5*/f32[512,8192]{1,0:T(8...) while((s32[]{:T(128)}, f32[2,512,128]{2,1,0:T(8,128)S(1)}, ...), condition=%wide.region_3.4_spmd, body=%wide.region_2.3_spmd.sunk | while | flops 805634048 | bytes 12846105 | solution.py:69
  756.6 51.6 %all-gather.17.cloned.1.call-done = f32[4096,128]{1,0:T(8,128)} async-done(((f32[512,128]{1,0:T(8,128)}), f32[4096,128]{1,0:T(8,128)}) %all-gather.17.cloned.1.call-update) | async-done | bytes 2097168 | tf_op jit(solution)/shard_map/while/body/eval_jaxpr/all_gather | solution.py:8
  814.6 51.6 %all-gather.17.cloned.1.call-done = f32[4096,128]{1,0:T(8,128)} async-done(((f32[512,128]{1,0:T(8,128)}), f32[4096,128]{1,0:T(8,128)}) %all-gather.17.cloned.1.call-update) | async-done | bytes 2097168 | tf_op jit(solution)/shard_map/while/body/eval_jaxpr/all_gather | solution.py:8
  872.6 51.6 %all-gather.17.cloned.1.call-done = f32[4096,128]{1,0:T(8,128)} async-done(((f32[512,128]{1,0:T(8,128)}), f32[4096,128]{1,0:T(8,128)}) %all-gather.17.cloned.1.call-update) | async-done | bytes 2097168 | tf_op jit(solution)/shard_map/while/body/eval_jaxpr/all_gather | solution.py:8
  930.6 51.6 %all-gather.17.cloned.1.call-done = f32[4096,128]{1,0:T(8,128)} async-done(((f32[512,128]{1,0:T(8,128)}), f32[4096,128]{1,0:T(8,128)}) %all-gather.17.cloned.1.call-update) | async-done | bytes 2097168 | tf_op jit(solution)/shard_map/while/body/eval_jaxpr/all_gather | solution.py:8
  988.6 51.6 %all-gather.17.cloned.1.call-done = f32[4096,128]{1,0:T(8,128)} async-done(((f32[512,128]{1,0:T(8,128)}), f32[4096,128]{1,0:T(8,128)}) %all-gather.17.cloned.1.call-update) | async-done | bytes 2097168 | tf_op jit(solution)/shard_map/while/body/eval_jaxpr/all_gather | solution.py:8
  1046.6 51.6 %all-gather.17.cloned.1.call-done = f32[4096,128]{1,0:T(8,128)} async-done(((f32[512,128]{1,0:T(8,128)}), f32[4096,128]{1,0:T(8,128)}) %all-gather.17.cloned.1.call-update) | async-done | bytes 2097168 | tf_op jit(solution)/shard_map/while/body/eval_jaxpr/all_gather | solution.py:8
  1104.6 51.6 %all-gather.17.cloned.1.call-done = f32[4096,128]{1,0:T(8,128)} async-done(((f32[512,128]{1,0:T(8,128)}), f32[4096,128]{1,0:T(8,128)}) %all-gather.17.cloned.1.call-update) | async-done | bytes 2097168 | tf_op jit(solution)/shard_map/while/body/eval_jaxpr/all_gather | solution.py:8
  1162.6 51.6 %all-gather.17.cloned.1.call-done = f32[4096,128]{1,0:T(8,128)} async-done(((f32[512,128]{1,0:T(8,128)}), f32[4096,128]{1,0:T(8,128)}) %all-gather.17.cloned.1.call-update) | async-done | bytes 2097168 | tf_op jit(solution)/shard_map/while/body/eval_jaxpr/all_gather | solution.py:8
  (155 shorter events, 156.3 us)
Async XLA Ops:
  6.5 1.6 copy-start.1
  6.5 181.1 %all-gather.13.cloned.1.call-start = ((), (), s32[]{:S(2)}) async-start(), calls=%async_computation.2 | async-start | bytes 35651584 | tf_op jit(solution)/shard_map/all_gather | solution.py:54
  7.3 274.3 %all-gather.11.cloned.1.call-start = ((), (), s32[]{:S(2)}) async-start(), calls=%async_computation.1 | async-start | bytes 17825792 | tf_op jit(solution)/shard_map/all_gather | solution.py:55
  65.7 1.5 copy-start.2
  71.1 20.0 %all-to-all-start = ((f32[16,1,8192]{2,1,0:T(1,128)}), f32[16,1,8192]{2,1,0:T(1,128)S(1)}, u32[]{:S(2)}, u32[]{:S(2)}) async-start(f32[16,1,8192]{2,1,0:T(1,128)} %reshape.83), calls=%async_computation | async-start | bytes 1048576 | tf_op jit(solution)/shard_map/all_to_all | solution.py:20
  281.6 57.7 %all-gather.15.cloned.1.call-start = ((), (), s32[]{:S(2)}) async-start(), calls=%async_computation.3 | async-start | bytes 2359296 | tf_op jit(solution)/shard_map/while/body/eval_jaxpr/all_gather | solution.py:8
  343.3 54.6 %all-gather.15.cloned.1.call-start = ((), (), s32[]{:S(2)}) async-start(), calls=%async_computation.3 | async-start | bytes 2359296 | tf_op jit(solution)/shard_map/while/body/eval_jaxpr/all_gather | solution.py:8
  401.9 54.6 %all-gather.15.cloned.1.call-start = ((), (), s32[]{:S(2)}) async-start(), calls=%async_computation.3 | async-start | bytes 2359296 | tf_op jit(solution)/shard_map/while/body/eval_jaxpr/all_gather | solution.py:8
  460.5 54.6 %all-gather.15.cloned.1.call-start = ((), (), s32[]{:S(2)}) async-start(), calls=%async_computation.3 | async-start | bytes 2359296 | tf_op jit(solution)/shard_map/while/body/eval_jaxpr/all_gather | solution.py:8
  519.1 54.7 %all-gather.15.cloned.1.call-start = ((), (), s32[]{:S(2)}) async-start(), calls=%async_computation.3 | async-start | bytes 2359296 | tf_op jit(solution)/shard_map/while/body/eval_jaxpr/all_gather | solution.py:8
  577.7 54.6 %all-gather.15.cloned.1.call-start = ((), (), s32[]{:S(2)}) async-start(), calls=%async_computation.3 | async-start | bytes 2359296 | tf_op jit(solution)/shard_map/while/body/eval_jaxpr/all_gather | solution.py:8
  636.3 54.6 %all-gather.15.cloned.1.call-start = ((), (), s32[]{:S(2)}) async-start(), calls=%async_computation.3 | async-start | bytes 2359296 | tf_op jit(solution)/shard_map/while/body/eval_jaxpr/all_gather | solution.py:8
  694.9 54.6 %all-gather.15.cloned.1.call-start = ((), (), s32[]{:S(2)}) async-start(), calls=%async_computation.3 | async-start | bytes 2359296 | tf_op jit(solution)/shard_map/while/body/eval_jaxpr/all_gather | solution.py:8
  753.6 54.6 %all-gather.17.cloned.1.call-start = ((), (), s32[]{:S(2)}) async-start(), calls=%async_computation.4 | async-start | bytes 2359296 | tf_op jit(solution)/shard_map/while/body/eval_jaxpr/all_gather | solution.py:8
  811.6 54.6 %all-gather.17.cloned.1.call-start = ((), (), s32[]{:S(2)}) async-start(), calls=%async_computation.4 | async-start | bytes 2359296 | tf_op jit(solution)/shard_map/while/body/eval_jaxpr/all_gather | solution.py:8
  869.5 54.7 %all-gather.17.cloned.1.call-start = ((), (), s32[]{:S(2)}) async-start(), calls=%async_computation.4 | async-start | bytes 2359296 | tf_op jit(solution)/shard_map/while/body/eval_jaxpr/all_gather | solution.py:8
  927.6 54.6 %all-gather.17.cloned.1.call-start = ((), (), s32[]{:S(2)}) async-start(), calls=%async_computation.4 | async-start | bytes 2359296 | tf_op jit(solution)/shard_map/while/body/eval_jaxpr/all_gather | solution.py:8
  985.5 54.6 %all-gather.17.cloned.1.call-start = ((), (), s32[]{:S(2)}) async-start(), calls=%async_computation.4 | async-start | bytes 2359296 | tf_op jit(solution)/shard_map/while/body/eval_jaxpr/all_gather | solution.py:8
  1043.5 54.6 %all-gather.17.cloned.1.call-start = ((), (), s32[]{:S(2)}) async-start(), calls=%async_computation.4 | async-start | bytes 2359296 | tf_op jit(solution)/shard_map/while/body/eval_jaxpr/all_gather | solution.py:8
  1101.5 54.6 %all-gather.17.cloned.1.call-start = ((), (), s32[]{:S(2)}) async-start(), calls=%async_computation.4 | async-start | bytes 2359296 | tf_op jit(solution)/shard_map/while/body/eval_jaxpr/all_gather | solution.py:8
  1159.5 54.6 %all-gather.17.cloned.1.call-start = ((), (), s32[]{:S(2)}) async-start(), calls=%async_computation.4 | async-start | bytes 2359296 | tf_op jit(solution)/shard_map/while/body/eval_jaxpr/all_gather | solution.py:8
  1217.5 0.8 copy-start
Sparse Core Ops, SparseCore 0:
  9.0 178.6 all-gather.12
  189.3 92.2 all-gather.10
  284.7 54.5 all-gather.14
  346.4 51.4 all-gather.14
  405.0 51.4 all-gather.14
  463.6 51.4 all-gather.14
  522.2 51.4 all-gather.14
  580.9 51.4 all-gather.14
  639.5 51.4 all-gather.14
  698.1 51.4 all-gather.14
  756.7 51.4 all-gather.16
  814.7 51.4 all-gather.16
  872.7 51.4 all-gather.16
  930.7 51.4 all-gather.16
  988.7 51.4 all-gather.16
  1046.7 51.4 all-gather.16
  1104.7 51.4 all-gather.16
  1162.7 51.4 all-gather.16
where the time goes:
time: 1230 us
  waiting for transfers between devices  1000 us (81%)
  matrix products  94.2 us (8%)
  other arithmetic  59.8 us (5%)
  local copies, waits for them, and re-layouts  45.9 us (4%)
  between operations  13.6 us (1%)
    all_gather x16, waiting for transfers between devices, picked(): lax.all_gather(array, axis)  814 us
    all_gather x1, waiting for transfers between devices, on_device(): lax.all_gather(tri_panels, 'col', axis=1, tiled=True)  91.5 us
    all_gather x1, waiting for transfers between devices, on_device(): lax.all_gather(own_inverse, 'col', axis=1, tiled=True)  82.4 us
    dot_general x16, matrix products, advance(): jnp.dot(inverse_block, current, precision=lax.Precision.HIGHEST, preferre...  46.7 us
    dot_general x16, matrix products, advance(): jnp.einsum('sij,jc->sic', pieces, solution, precision=lax.Precision.HIGHEST)  41.8 us
    another operation x4, other arithmetic, on_device(): jax.scipy.linalg.solve_triangular(own_diag, identity_block, lower=True)  41.5 us
  transfers between devices with their start and end apart: 19, of which 19 were waited for; matrix products, arithmetic and copies ran while one was open for 8% of the time, Pallas kernels for 0%

commit v1 on v0

--- a/solution.py
+++ b/solution.py
@@ -52,7 +52,7 @@
     group_count = (col_count + row_count - 1) // row_count
     everything, inverses = (
         lax.all_gather(tri_panels, "col", axis=1, tiled=True),
-        lax.all_gather(own_inverse, "col", axis=1, tiled=True),
+        jnp.concatenate(lax.all_gather(own_inverse, "col"), axis=1),
     )
     for first_slot in range(group_count):
         begin_step = first_slot * row_count

time: 1230 us -> 1290 us (1.049)
  waiting for transfers between devices: 1000 us -> 1060 us
    all_gather x1, waiting for transfers between devices: 91.5 us -> 161 us  [on_device(): lax.all_gather(tri_panels, 'col', axis=1, tiled=True)]
  transfers between devices with their start and end apart: 19 -> 19, of which waited for: 19 -> 19; matrix products, arithmetic and copies ran while one was open for 8% -> 3% of each run, Pallas kernels for 0% -> 0%
where the time goes in v1:
time: 1290 us
  waiting for transfers between devices  1060 us (82%)
  matrix products  91.5 us (7%)
  other arithmetic  60 us (5%)
  local copies, waits for them, and re-layouts  53.8 us (4%)
  between operations  13.6 us (1%)
    all_gather x16, waiting for transfers between devices, picked(): lax.all_gather(array, axis)  814 us
    all_gather x1, waiting for transfers between devices, on_device(): lax.all_gather(tri_panels, 'col', axis=1, tiled=True)  161 us
    all_gather x1, waiting for transfers between devices, on_device(): lax.all_gather(own_inverse, 'col')  70.5 us
    dot_general x16, matrix products, advance(): jnp.dot(inverse_block, current, precision=lax.Precision.HIGHEST, preferre...  46.7 us
    dot_general x16, matrix products, advance(): jnp.einsum('sij,jc->sic', pieces, solution, precision=lax.Precision.HIGHEST)  41.8 us
    another operation x4, other arithmetic, on_device(): jax.scipy.linalg.solve_triangular(own_diag, identity_block, lower=True)  41.7 us
  transfers between devices with their start and end apart: 19, of which 19 were waited for; matrix products, arithmetic and copies ran while one was open for 3% of the time, Pallas kernels for 0%

profile of v1, /device:TPU:0, one launch (start us, length us, event | category | flops | bytes accessed | tf_op | source)
XLA Modules:
  0.0 1287.5 jit_solution(2364498989049787948)
XLA Ops:
  16.2 39.3 %custom-call.4 = f32[4,128,128]{1,2,0:T(8,128)S(1)} custom-call(f32[4,128,128]{2,1,0:T(8,128)S(1)} %get-tuple-element.290), custom_call_target="InvertDiagBlocksLowerTriangular" | custom-call | tf_op jit(solution)/shard_map/jit(_solve_triangular)/triangular_solve | solution.py:25
  70.1 13.7 %all-to-all-done = f32[16,1,8192]{2,1,0:T(1,128)S(1)} async-done(((f32[16,1,8192]{2,1,0:T(1,128)}), f32[16,1,8192]{2,1,0:T(1,128)S(1)}, u32[]{:S(2)}, u32[]{:S(2)}) %all-to-all-start) | async-done | bytes 524320 | tf_op jit(solution)/shard_map/all_to_all | solution.py:20
  88.9 70.5 %all-gather.14.cloned.1.call-done = f32[8192,512]{1,0:T(8,128)} async-done(((f32[512,512]{1,0:T(8,128)}), f32[8192,512]{1,0:T(8,128)}) %all-gather.14.cloned.1.call-update) | async-done | bytes 16777232 | tf_op jit(solution)/shard_map/all_gather | solution.py:55
  159.3 12.0 copy.17
  171.3 161.2 %all-gather.12.cloned.1.call-done = f32[1024,8192]{1,0:T(8,128)} async-done(((f32[1024,512]{1,0:T(8,128)}), f32[1024,8192]{1,0:T(8,128)}) %all-gather.12.cloned.1.call-update) | async-done | bytes 33554448 | tf_op jit(solution)/shard_map/all_gather | solution.py:54
  332.5 11.5 slice.70
  344.0 471.8 %while.31 = (s32[]{:T(128)}, f32[2,512,128]{2,1,0:T(8,128)S(1)}, s32[]{:T(128)}, f32[512,8192]{1,0:T(8,128)}, f32[1024,8192]{1,0:T(8,128)}, /*index=5*/s32[]{:T(...) while((s32[]{:T(128)}, f32[2,512,128]{2,1,0:T(8,128)S(1)}, ...), condition=%wide.region_1.2_spmd, body=%wide.region_0.1_spmd.sunk | while | flops 1208287232 | bytes 17039816 | solution.py:69
  348.7 52.9 %all-gather.16.cloned.1.call-done = f32[4096,128]{1,0:T(8,128)} async-done(((f32[512,128]{1,0:T(8,128)}), f32[4096,128]{1,0:T(8,128)}) %all-gather.16.cloned.1.call-update) | async-done | bytes 2097168 | tf_op jit(solution)/shard_map/while/body/eval_jaxpr/all_gather | solution.py:8
  410.4 49.8 %all-gather.16.cloned.1.call-done = f32[4096,128]{1,0:T(8,128)} async-done(((f32[512,128]{1,0:T(8,128)}), f32[4096,128]{1,0:T(8,128)}) %all-gather.16.cloned.1.call-update) | async-done | bytes 2097168 | tf_op jit(solution)/shard_map/while/body/eval_jaxpr/all_gather | solution.py:8
  469.0 49.8 %all-gather.16.cloned.1.call-done = f32[4096,128]{1,0:T(8,128)} async-done(((f32[512,128]{1,0:T(8,128)}), f32[4096,128]{1,0:T(8,128)}) %all-gather.16.cloned.1.call-update) | async-done | bytes 2097168 | tf_op jit(solution)/shard_map/while/body/eval_jaxpr/all_gather | solution.py:8
  527.6 49.8 %all-gather.16.cloned.1.call-done = f32[4096,128]{1,0:T(8,128)} async-done(((f32[512,128]{1,0:T(8,128)}), f32[4096,128]{1,0:T(8,128)}) %all-gather.16.cloned.1.call-update) | async-done | bytes 2097168 | tf_op jit(solution)/shard_map/while/body/eval_jaxpr/all_gather | solution.py:8
  586.2 49.8 %all-gather.16.cloned.1.call-done = f32[4096,128]{1,0:T(8,128)} async-done(((f32[512,128]{1,0:T(8,128)}), f32[4096,128]{1,0:T(8,128)}) %all-gather.16.cloned.1.call-update) | async-done | bytes 2097168 | tf_op jit(solution)/shard_map/while/body/eval_jaxpr/all_gather | solution.py:8
  644.8 49.8 %all-gather.16.cloned.1.call-done = f32[4096,128]{1,0:T(8,128)} async-done(((f32[512,128]{1,0:T(8,128)}), f32[4096,128]{1,0:T(8,128)}) %all-gather.16.cloned.1.call-update) | async-done | bytes 2097168 | tf_op jit(solution)/shard_map/while/body/eval_jaxpr/all_gather | solution.py:8
  703.4 49.8 %all-gather.16.cloned.1.call-done = f32[4096,128]{1,0:T(8,128)} async-done(((f32[512,128]{1,0:T(8,128)}), f32[4096,128]{1,0:T(8,128)}) %all-gather.16.cloned.1.call-update) | async-done | bytes 2097168 | tf_op jit(solution)/shard_map/while/body/eval_jaxpr/all_gather | solution.py:8
  762.1 49.8 %all-gather.16.cloned.1.call-done = f32[4096,128]{1,0:T(8,128)} async-done(((f32[512,128]{1,0:T(8,128)}), f32[4096,128]{1,0:T(8,128)}) %all-gather.16.cloned.1.call-update) | async-done | bytes 2097168 | tf_op jit(solution)/shard_map/while/body/eval_jaxpr/all_gather | solution.py:8
  815.8 464.0 %while.32 = (s32[]{:T(128)}, f32[2,512,128]{2,1,0:T(8,128)S(1)}, s32[]{:T(128)}, f32[512,8192]{1,0:T(8,128)}, s32[1]{0:T(128)}, /*index=5*/f32[512,8192]{1,0:T(8...) while((s32[]{:T(128)}, f32[2,512,128]{2,1,0:T(8,128)S(1)}, ...), condition=%wide.region_3.4_spmd, body=%wide.region_2.3_spmd.sunk | while | flops 805634048 | bytes 12846105 | solution.py:69
  818.9 51.6 %all-gather.18.cloned.1.call-done = f32[4096,128]{1,0:T(8,128)} async-done(((f32[512,128]{1,0:T(8,128)}), f32[4096,128]{1,0:T(8,128)}) %all-gather.18.cloned.1.call-update) | async-done | bytes 2097168 | tf_op jit(solution)/shard_map/while/body/eval_jaxpr/all_gather | solution.py:8
  876.9 51.6 %all-gather.18.cloned.1.call-done = f32[4096,128]{1,0:T(8,128)} async-done(((f32[512,128]{1,0:T(8,128)}), f32[4096,128]{1,0:T(8,128)}) %all-gather.18.cloned.1.call-update) | async-done | bytes 2097168 | tf_op jit(solution)/shard_map/while/body/eval_jaxpr/all_gather | solution.py:8
  934.9 51.6 %all-gather.18.cloned.1.call-done = f32[4096,128]{1,0:T(8,128)} async-done(((f32[512,128]{1,0:T(8,128)}), f32[4096,128]{1,0:T(8,128)}) %all-gather.18.cloned.1.call-update) | async-done | bytes 2097168 | tf_op jit(solution)/shard_map/while/body/eval_jaxpr/all_gather | solution.py:8
  992.9 51.6 %all-gather.18.cloned.1.call-done = f32[4096,128]{1,0:T(8,128)} async-done(((f32[512,128]{1,0:T(8,128)}), f32[4096,128]{1,0:T(8,128)}) %all-gather.18.cloned.1.call-update) | async-done | bytes 2097168 | tf_op jit(solution)/shard_map/while/body/eval_jaxpr/all_gather | solution.py:8
  1050.9 51.6 %all-gather.18.cloned.1.call-done = f32[4096,128]{1,0:T(8,128)} async-done(((f32[512,128]{1,0:T(8,128)}), f32[4096,128]{1,0:T(8,128)}) %all-gather.18.cloned.1.call-update) | async-done | bytes 2097168 | tf_op jit(solution)/shard_map/while/body/eval_jaxpr/all_gather | solution.py:8
  1108.9 51.6 %all-gather.18.cloned.1.call-done = f32[4096,128]{1,0:T(8,128)} async-done(((f32[512,128]{1,0:T(8,128)}), f32[4096,128]{1,0:T(8,128)}) %all-gather.18.cloned.1.call-update) | async-done | bytes 2097168 | tf_op jit(solution)/shard_map/while/body/eval_jaxpr/all_gather | solution.py:8
  1166.9 51.6 %all-gather.18.cloned.1.call-done = f32[4096,128]{1,0:T(8,128)} async-done(((f32[512,128]{1,0:T(8,128)}), f32[4096,128]{1,0:T(8,128)}) %all-gather.18.cloned.1.call-update) | async-done | bytes 2097168 | tf_op jit(solution)/shard_map/while/body/eval_jaxpr/all_gather | solution.py:8
  1224.9 51.6 %all-gather.18.cloned.1.call-done = f32[4096,128]{1,0:T(8,128)} async-done(((f32[512,128]{1,0:T(8,128)}), f32[4096,128]{1,0:T(8,128)}) %all-gather.18.cloned.1.call-update) | async-done | bytes 2097168 | tf_op jit(solution)/shard_map/while/body/eval_jaxpr/all_gather | solution.py:8
  (154 shorter events, 157.8 us)
Async XLA Ops:
  6.5 152.8 %all-gather.14.cloned.1.call-start = ((), (), s32[]{:S(2)}) async-start(), calls=%async_computation.2 | async-start | bytes 17825792 | tf_op jit(solution)/shard_map/all_gather | solution.py:55
  59.7 1.0 copy-start.1
  59.7 272.8 %all-gather.12.cloned.1.call-start = ((), (), s32[]{:S(2)}) async-start(), calls=%async_computation.1 | async-start | bytes 35651584 | tf_op jit(solution)/shard_map/all_gather | solution.py:54
  64.6 19.2 %all-to-all-start = ((f32[16,1,8192]{2,1,0:T(1,128)}), f32[16,1,8192]{2,1,0:T(1,128)S(1)}, u32[]{:S(2)}, u32[]{:S(2)}) async-start(f32[16,1,8192]{2,1,0:T(1,128)} %reshape.92), calls=%async_computation | async-start | bytes 1048576 | tf_op jit(solution)/shard_map/all_to_all | solution.py:20
  344.0 57.6 %all-gather.16.cloned.1.call-start = ((), (), s32[]{:S(2)}) async-start(), calls=%async_computation.3 | async-start | bytes 2359296 | tf_op jit(solution)/shard_map/while/body/eval_jaxpr/all_gather | solution.py:8
  405.6 54.6 %all-gather.16.cloned.1.call-start = ((), (), s32[]{:S(2)}) async-start(), calls=%async_computation.3 | async-start | bytes 2359296 | tf_op jit(solution)/shard_map/while/body/eval_jaxpr/all_gather | solution.py:8
  464.2 54.6 %all-gather.16.cloned.1.call-start = ((), (), s32[]{:S(2)}) async-start(), calls=%async_computation.3 | async-start | bytes 2359296 | tf_op jit(solution)/shard_map/while/body/eval_jaxpr/all_gather | solution.py:8
  522.8 54.6 %all-gather.16.cloned.1.call-start = ((), (), s32[]{:S(2)}) async-start(), calls=%async_computation.3 | async-start | bytes 2359296 | tf_op jit(solution)/shard_map/while/body/eval_jaxpr/all_gather | solution.py:8
  581.4 54.7 %all-gather.16.cloned.1.call-start = ((), (), s32[]{:S(2)}) async-start(), calls=%async_computation.3 | async-start | bytes 2359296 | tf_op jit(solution)/shard_map/while/body/eval_jaxpr/all_gather | solution.py:8
  640.0 54.6 %all-gather.16.cloned.1.call-start = ((), (), s32[]{:S(2)}) async-start(), calls=%async_computation.3 | async-start | bytes 2359296 | tf_op jit(solution)/shard_map/while/body/eval_jaxpr/all_gather | solution.py:8
  698.6 54.6 %all-gather.16.cloned.1.call-start = ((), (), s32[]{:S(2)}) async-start(), calls=%async_computation.3 | async-start | bytes 2359296 | tf_op jit(solution)/shard_map/while/body/eval_jaxpr/all_gather | solution.py:8
  757.2 54.6 %all-gather.16.cloned.1.call-start = ((), (), s32[]{:S(2)}) async-start(), calls=%async_computation.3 | async-start | bytes 2359296 | tf_op jit(solution)/shard_map/while/body/eval_jaxpr/all_gather | solution.py:8
  815.9 54.6 %all-gather.18.cloned.1.call-start = ((), (), s32[]{:S(2)}) async-start(), calls=%async_computation.4 | async-start | bytes 2359296 | tf_op jit(solution)/shard_map/while/body/eval_jaxpr/all_gather | solution.py:8
  873.9 54.6 %all-gather.18.cloned.1.call-start = ((), (), s32[]{:S(2)}) async-start(), calls=%async_computation.4 | async-start | bytes 2359296 | tf_op jit(solution)/shard_map/while/body/eval_jaxpr/all_gather | solution.py:8
  931.8 54.7 %all-gather.18.cloned.1.call-start = ((), (), s32[]{:S(2)}) async-start(), calls=%async_computation.4 | async-start | bytes 2359296 | tf_op jit(solution)/shard_map/while/body/eval_jaxpr/all_gather | solution.py:8
  989.9 54.6 %all-gather.18.cloned.1.call-start = ((), (), s32[]{:S(2)}) async-start(), calls=%async_computation.4 | async-start | bytes 2359296 | tf_op jit(solution)/shard_map/while/body/eval_jaxpr/all_gather | solution.py:8
  1047.8 54.6 %all-gather.18.cloned.1.call-start = ((), (), s32[]{:S(2)}) async-start(), calls=%async_computation.4 | async-start | bytes 2359296 | tf_op jit(solution)/shard_map/while/body/eval_jaxpr/all_gather | solution.py:8
  1105.8 54.6 %all-gather.18.cloned.1.call-start = ((), (), s32[]{:S(2)}) async-start(), calls=%async_computation.4 | async-start | bytes 2359296 | tf_op jit(solution)/shard_map/while/body/eval_jaxpr/all_gather | solution.py:8
  1163.8 54.6 %all-gather.18.cloned.1.call-start = ((), (), s32[]{:S(2)}) async-start(), calls=%async_computation.4 | async-start | bytes 2359296 | tf_op jit(solution)/shard_map/while/body/eval_jaxpr/all_gather | solution.py:8
  1221.8 54.6 %all-gather.18.cloned.1.call-start = ((), (), s32[]{:S(2)}) async-start(), calls=%async_computation.4 | async-start | bytes 2359296 | tf_op jit(solution)/shard_map/while/body/eval_jaxpr/all_gather | solution.py:8
  1279.8 0.8 copy-start
Sparse Core Ops, SparseCore 0:
  59.8 99.4 all-gather.13
  161.0 171.4 all-gather.11
  347.1 54.4 all-gather.15
  408.7 51.4 all-gather.15
  467.3 51.4 all-gather.15
  525.9 51.4 all-gather.15
  584.5 51.4 all-gather.15
  643.2 51.4 all-gather.15
  701.8 51.4 all-gather.15
  760.4 51.4 all-gather.15
  819.0 51.4 all-gather.17
  877.0 51.4 all-gather.17
  935.0 51.4 all-gather.17
  993.0 51.4 all-gather.17
  1051.0 51.4 all-gather.17
  1109.0 51.4 all-gather.17
  1167.0 51.4 all-gather.17
  1225.0 51.4 all-gather.17
